TPU v7x, 32 devices: a whole 2x2x4 slice. The times are simulated.
32 devices in a mesh: row: 2 (over y), col: 16 (over z, x, core).
Axes of the slice: x: 2, y: 2, z: 4, core: 2. Of those that a mesh axis runs over, the one named last changes fastest.
Arguments:
- previous: bfloat16 [4, 32, 128, 256], P(None, 'row', 'col'), may hold values from -6 to 6
- skip_coarse: bfloat16 [4, 32, 128, 256], P(None, 'row', 'col'), may hold values from -6 to 6
- skip_fine: bfloat16 [4, 64, 256, 256], P(None, 'row', 'col'), may hold values from -6 to 6
- coarse_convs: bfloat16 [4, 3, 3, 256, 256], replicated, may hold values from -0.125 to 0.125
- coarse_biases: float32 [4, 256], replicated, may hold values from -3 to 3
- coarse_project: bfloat16 [256, 256], replicated, may hold values from -0.375 to 0.375
- coarse_offset: float32 [256], replicated, may hold values from -3 to 3
- fine_convs: bfloat16 [4, 3, 3, 256, 256], replicated, may hold values from -0.125 to 0.125
- fine_biases: float32 [4, 256], replicated, may hold values from -3 to 3
- fine_project: bfloat16 [256, 256], replicated, may hold values from -0.375 to 0.375
- fine_offset: float32 [256], replicated, may hold values from -3 to 3
Outputs:
- decoded: bfloat16 [4, 128, 512, 256], P(None, 'row', 'col')
All inputs are finite; a program needn't handle non-finite values.
Results may differ from a plain program's by a relative error of at most 0.012.
Values may be sent and summed in bfloat16 or wider, within the bound.
A program may use at most 128 MiB of HBM per device.

v0:
```python
import functools

import jax
import jax.numpy as jnp
import numpy as np
from jax import lax
from jax.experimental import pallas as pl
from jax.experimental.pallas import tpu as pltpu
from jax.sharding import PartitionSpec as P

SUB = 16
BF = jnp.bfloat16
F32 = jnp.float32
DIRECTIONS = ((0, -1), (0, 1), (-1, 0), (1, 0), (-1, -1), (-1, 1), (1, -1), (1, 1))


def roll(value, shift):
    shift = shift % SUB
    if shift == 0:
        return value
    axis = value.ndim - 2
    if value.ndim == 3:
        return jnp.concatenate([value[:, SUB - shift :], value[:, : SUB - shift]], axis=1)
    return jnp.concatenate([value[SUB - shift :], value[: SUB - shift]], axis=axis)


class Level:
    def __init__(self, images, stage, packed, landed, corners, send, recv):
        self.image = images.at[stage]
        self.packed = packed.at[stage]
        self.landed = landed.at[stage]
        self.corners = corners.at[stage]
        self.send = send.at[stage]
        self.recv = recv.at[stage]
        self.rows = images.shape[1] - 2
        self.cols = images.shape[2] - 2


class Place:
    def __init__(self):
        self.row = lax.axis_index("row")
        self.col = lax.axis_index("col")
        self.rows = lax.axis_size("row")
        self.cols = lax.axis_size("col")

    def has(self, dr, dc):
        ok = None
        tests = []
        if dr == -1:
            tests.append(self.row > 0)
        if dr == 1:
            tests.append(self.row < self.rows - 1)
        if dc == -1:
            tests.append(self.col > 0)
        if dc == 1:
            tests.append(self.col < self.cols - 1)
        for test in tests:
            ok = test if ok is None else jnp.logical_and(ok, test)
        return ok

    def peers(self):
        def around(index, count):
            return 1 + (index > 0).astype(jnp.int32) + (index < count - 1).astype(jnp.int32)

        return around(self.row, self.rows) * around(self.col, self.cols) - 1

    def at(self, dr, dc):
        return (self.row + dr, self.col + dc)


def sub_index(shape):
    return lax.broadcasted_iota(jnp.int32, shape, len(shape) - 2)


def copies(place, lv):
    r, c = lv.rows, lv.cols
    im = lv.image
    ends = (
        (im.at[1 : r + 1, 1], im.at[1 : r + 1, c + 1]),
        (im.at[1 : r + 1, c], im.at[1 : r + 1, 0]),
        (lv.packed.at[0], lv.landed.at[1]),
        (lv.packed.at[1], lv.landed.at[0]),
        (im.at[1, 1], lv.corners.at[3]),
        (im.at[1, c], lv.corners.at[2]),
        (im.at[r, 1], lv.corners.at[1]),
        (im.at[r, c], lv.corners.at[0]),
    )
    return [
        pltpu.make_async_remote_copy(
            src_ref=src,
            dst_ref=dst,
            send_sem=lv.send.at[i],
            recv_sem=lv.recv.at[i],
            device_id=place.at(*DIRECTIONS[i]),
            device_id_type=pl.DeviceIdType.MESH,
        )
        for i, (src, dst) in enumerate(ends)
    ]


def exchange(place, lv, batch):
    r, c = lv.rows, lv.cols
    groups = SUB // batch
    channels = lv.image.shape[-1]
    moves = copies(place, lv)
    for i in (0, 1):
        pl.when(place.has(*DIRECTIONS[i]))(moves[i].start)
    slot = sub_index((c // groups, SUB, channels)) // batch
    for side, row in ((0, 1), (1, r)):
        v = lv.image[row, 1 : c + 1].astype(F32).reshape(c // groups, groups, SUB, channels)
        total = None
        for q in range(groups):
            part = roll(v[:, q], batch * (q if side == 0 else q + 1))
            total = part if total is None else jnp.where(slot == q, part, total)
        lv.packed[side] = total.astype(BF)
    for i in range(2, 8):
        pl.when(place.has(*DIRECTIONS[i]))(moves[i].start)


def settle(place, lv, batch, replicate):
    r, c = lv.rows, lv.cols
    im, landed, corners = lv.image, lv.landed, lv.corners
    groups = SUB // batch
    channels = im.shape[-1]
    moves = copies(place, lv)
    for i, (dr, dc) in enumerate(DIRECTIONS):
        pl.when(place.has(dr, dc))(moves[i].wait_send)
        pl.when(place.has(-dr, -dc))(moves[i].wait_recv)

    no_up = place.row == 0
    no_down = place.row == place.rows - 1
    no_left = place.col == 0
    no_right = place.col == place.cols - 1

    def rolled(tile, shift):
        return roll(tile.astype(F32), shift).astype(BF)

    for missing, at, edge in ((no_left, 0, 1), (no_right, c + 1, c)):

        @pl.when(missing)
        def _(at=at, edge=edge):
            if replicate:
                im[1 : r + 1, at] = im[1 : r + 1, edge]
            else:
                im[1 : r + 1, at] = jnp.zeros((r, SUB, channels), BF)

    for side, missing in ((0, no_up), (1, no_down)):

        @pl.when(missing)
        def _(side=side):
            if replicate:
                landed[side] = lv.packed[side]
            else:
                landed[side] = jnp.zeros((c // groups, SUB, channels), BF)

    last = c // groups - 1
    for k, vertical, horizontal in (
        (0, no_up, no_left),
        (1, no_up, no_right),
        (2, no_down, no_left),
        (3, no_down, no_right),
    ):
        if not replicate:

            @pl.when(jnp.logical_or(vertical, horizontal))
            def _(k=k):
                corners[k] = jnp.zeros((SUB, channels), BF)

        else:
            side = k // 2
            turn = -batch if side == 0 else batch
            row = 1 if side == 0 else r
            col = 0 if k % 2 == 0 else c + 1

            @pl.when(vertical)
            def _(k=k, turn=turn, row=row, col=col):
                corners[k] = rolled(im[row, col], turn)

            shift = (-batch, 0, 0, batch)[k]
            block = 0 if k % 2 == 0 else last

            @pl.when(jnp.logical_and(jnp.logical_not(vertical), horizontal))
            def _(k=k, side=side, shift=shift, block=block):
                corners[k] = rolled(landed[side, block], shift)

    group = sub_index((c + 2, SUB, channels)) // batch
    for side in (0, 1):
        near = roll(im[r if side == 0 else 1].astype(F32), batch if side == 0 else -batch)
        wide = landed[side].astype(F32)
        parts = [
            roll(wide, -batch * q if side == 0 else batch * (groups - 1 - q))
            for q in range(groups)
        ]
        inner = jnp.stack(parts, axis=1).reshape(c, SUB, channels)
        turn = batch if side == 0 else -batch
        ends = [
            roll(corners[2 * side + k].astype(F32), turn).reshape(1, SUB, channels) for k in (0, 1)
        ]
        outer = jnp.concatenate([ends[0], inner, ends[1]], axis=0)
        chosen = 0 if side == 0 else groups - 1
        im[0 if side == 0 else r + 1] = jnp.where(group == chosen, outer, near).astype(BF)


def conv_rows(lv, weight, start, count):
    c = lv.cols
    channels = lv.image.shape[-1]
    taps = [
        lv.image[pl.ds(start + dr, count), dc : dc + c].reshape(count * c * SUB, channels)
        for dr in range(3)
        for dc in range(3)
    ]
    return jnp.dot(jnp.concatenate(taps, axis=1), weight[...], preferred_element_type=F32)


def body(
    batch,
    prev,
    skip_c,
    skip_f,
    cw_hbm,
    cb,
    cp,
    co,
    fw_hbm,
    fb,
    fp,
    perm_c,
    perm_f,
    out,
    ic,
    if_,
    pack_c,
    pack_f,
    land_c,
    land_f,
    corner_c,
    corner_f,
    cw,
    fw,
    xc,
    xf,
    sum_f,
    send_c,
    recv_c,
    send_f,
    recv_f,
    wsem,
):
    place = Place()
    channels = skip_c.shape[-1]
    loads = {}
    for i in range(4):
        for k, (src, dst) in enumerate(((cw_hbm, cw), (fw_hbm, fw))):
            loads[k, i] = pltpu.make_async_copy(src.at[i], dst.at[i], wsem.at[k, i])
    for key in ((0, 0), (1, 0), (0, 1), (1, 1), (0, 2), (0, 3), (1, 2), (1, 3)):
        loads[key].start()

    barrier = pltpu.get_barrier_semaphore()
    for d in DIRECTIONS:

        @pl.when(place.has(*d))
        def _(d=d):
            pl.semaphore_signal(
                barrier, inc=1, device_id=place.at(*d), device_id_type=pl.DeviceIdType.MESH
            )

    lc = [Level(ic, s, pack_c, land_c, corner_c, send_c, recv_c) for s in range(5)]
    lf = [Level(if_, s, pack_f, land_f, corner_f, send_f, recv_f) for s in range(5)]
    rc, cc, rf, cf = lc[0].rows, lc[0].cols, lf[0].rows, lf[0].cols

    def regroup(ref, perm, row):
        tile = ref[:, :, row].reshape(perm.shape[0], channels)
        return jnp.dot(perm[...], tile, preferred_element_type=F32).reshape(-1, SUB, channels)

    @pl.loop(0, rc)
    def _(row):
        v = regroup(skip_c, perm_c, row)
        xc[row] = v + regroup(prev, perm_c, row)
        ic[0, row + 1, 1 : cc + 1] = jnp.maximum(v, 0.0).astype(BF)


    pl.semaphore_wait(barrier, place.peers())

    exchange(place, lc[0], batch)

    @pl.loop(0, rf)
    def _(row):
        v = regroup(skip_f, perm_f, row)
        xf[row] = v.astype(BF)
        if_[0, row + 1, 1 : cf + 1] = jnp.maximum(v, 0.0).astype(BF)

    exchange(place, lf[0], batch)

    def coarse(stage, finish):
        settle(place, lc[stage], batch, False)
        loads[0, stage].wait()
        v = conv_rows(lc[stage], cw.at[stage], 0, rc) + cb[stage : stage + 1]
        v = finish(v.reshape(rc, cc, SUB, channels))
        lc[stage + 1].image[1 : rc + 1, 1 : cc + 1] = v
        exchange(place, lc[stage + 1], batch)

    step = 2 if rf % 2 == 0 else 1

    def fine(stage, finish, first, last):
        @pl.loop(first, last)
        def _(i):
            v = conv_rows(lf[stage], fw.at[stage], i * step, step) + fb[stage : stage + 1]
            finish(i * step, v.reshape(step, cf, SUB, channels))

    def fine_ready(stage):
        settle(place, lf[stage], batch, False)
        loads[1, stage].wait()

    def hidden(v):
        return jnp.maximum(v, 0.0).astype(BF)

    def summed(v):
        v = v + xc[...]
        xc[...] = v
        return jnp.maximum(v, 0.0).astype(BF)

    def lifted(v):
        top = (v + xc[...]).astype(BF).reshape(rc * cc * SUB, channels)
        z = jnp.dot(top, cp[...], preferred_element_type=F32)
        return z.astype(BF).reshape(rc, cc, SUB, channels)

    def keep_hidden(stage):
        def finish(row, v):
            if_[stage + 1, pl.ds(row + 1, step), 1 : cf + 1] = hidden(v)

        return finish

    def keep_unit(row, v):
        sum_f[pl.ds(row, step)] = v + xf[pl.ds(row, step)].astype(F32)

    def keep_top(row, v):
        top = (v + sum_f[pl.ds(row, step)]).astype(BF).reshape(step * cf * SUB, channels)
        z = jnp.dot(top, fp[...], preferred_element_type=F32)
        if_[4, pl.ds(row + 1, step), 1 : cf + 1] = z.astype(BF).reshape(step, cf, SUB, channels)

    steps = rf // step
    half = steps // 2
    coarse(0, hidden)
    fine_ready(0)
    fine(0, keep_hidden(0), 0, steps)
    exchange(place, lf[1], batch)
    coarse(1, summed)
    fine_ready(1)
    fine(1, keep_unit, 0, half)
    coarse(2, hidden)
    fine(1, keep_unit, half, steps)
    coarse(3, lifted)
    settle(place, lc[4], batch, True)

    @pl.loop(0, rc)
    def _(row):
        mid = 0.75 * ic[4, row + 1].astype(F32)
        for p in range(2):
            v = mid + 0.25 * ic[4, row + 2 * p].astype(F32)
            core = 0.75 * v[1 : cc + 1]
            even = core + 0.25 * v[0:cc]
            odd = core + 0.25 * v[2 : cc + 2]
            both = jnp.stack([even, odd], axis=1).reshape(cf, SUB, channels)
            joined = (both + co[...]).astype(BF).astype(F32)
            total = joined + sum_f[2 * row + p]
            sum_f[2 * row + p] = total
            if_[2, 2 * row + p + 1, 1 : cf + 1] = jnp.maximum(total, 0.0).astype(BF)

    exchange(place, lf[2], batch)
    fine_ready(2)
    fine(2, keep_hidden(2), 0, steps)
    exchange(place, lf[3], batch)
    fine_ready(3)
    fine(3, keep_top, 0, steps)
    exchange(place, lf[4], batch)
    settle(place, lf[4], batch, True)

    @pl.loop(0, rf + 2)
    def _(row):
        out[row] = if_[4, row]


def raise_body(batch, z, spread, offset, out):
    row = pl.program_id(0)
    channels = z.shape[-1]
    mid = 0.75 * z[row + 1].astype(F32)
    for p in range(2):
        v = (mid + 0.25 * z[row + 2 * p].astype(F32)).astype(BF).reshape(-1, channels)
        res = jnp.dot(spread[...], v, preferred_element_type=F32) + offset[...]
        out[:, :, p] = res.astype(BF).reshape(batch, SUB // batch, -1, channels)


def regroup_matrix(batch, cols):
    groups = SUB // batch
    m = np.zeros((cols, groups, batch, batch, groups, cols), np.float32)
    for c in range(cols):
        for g in range(groups):
            for b in range(batch):
                m[c, g, b, b, g, c] = 1.0
    return jnp.asarray(m.reshape(cols * SUB, cols * SUB), BF)


def spread_matrix(batch, cols):
    groups = SUB // batch
    m = np.zeros((batch, groups, 2 * cols, cols + 2, groups, batch), np.float32)
    for g in range(groups):
        for b in range(batch):
            for c in range(cols):
                m[b, g, 2 * c, c + 1, g, b] = 0.75
                m[b, g, 2 * c, c, g, b] = 0.25
                m[b, g, 2 * c + 1, c + 1, g, b] = 0.75
                m[b, g, 2 * c + 1, c + 2, g, b] = 0.25
    return jnp.asarray(m.reshape(SUB * 2 * cols, (cols + 2) * SUB), BF)


def per_device(prev, skip_c, skip_f, cw, cb, cp, co, fw, fb, fp, fo):
    batch, hc, cc, ch = prev.shape
    _, hf, cf, _ = skip_f.shape
    groups = SUB // batch
    rc, rf = hc // groups, hf // groups

    def grouped(v):
        return v.reshape(batch, groups, v.shape[1] // groups, v.shape[2], ch)

    vmem = pl.BlockSpec(memory_space=pltpu.VMEM)
    hbm = pl.BlockSpec(memory_space=pl.ANY)
    dma = pltpu.SemaphoreType.DMA
    z = pl.pallas_call(
        functools.partial(body, batch),
        out_shape=jax.ShapeDtypeStruct((rf + 2, cf + 2, SUB, ch), BF),
        in_specs=[vmem, vmem, vmem, hbm, vmem, vmem, vmem, hbm, vmem, vmem, vmem, vmem],
        out_specs=vmem,
        scratch_shapes=[
            pltpu.VMEM((5, rc + 2, cc + 2, SUB, ch), BF),
            pltpu.VMEM((5, rf + 2, cf + 2, SUB, ch), BF),
            pltpu.VMEM((5, 2, cc // groups, SUB, ch), BF),
            pltpu.VMEM((5, 2, cf // groups, SUB, ch), BF),
            pltpu.VMEM((5, 2, cc // groups, SUB, ch), BF),
            pltpu.VMEM((5, 2, cf // groups, SUB, ch), BF),
            pltpu.VMEM((5, 4, SUB, ch), BF),
            pltpu.VMEM((5, 4, SUB, ch), BF),
            pltpu.VMEM((4, 9 * ch, ch), BF),
            pltpu.VMEM((4, 9 * ch, ch), BF),
            pltpu.VMEM((rc, cc, SUB, ch), F32),
            pltpu.VMEM((rf, cf, SUB, ch), BF),
            pltpu.VMEM((rf, cf, SUB, ch), F32),
            dma((5, 8)),
            dma((5, 8)),
            dma((5, 8)),
            dma((5, 8)),
            dma((2, 4)),
        ],
        compiler_params=pltpu.CompilerParams(
            collective_id=0, has_side_effects=True, vmem_limit_bytes=60 * 1024 * 1024
        ),
    )(
        grouped(prev),
        grouped(skip_c),
        grouped(skip_f),
        cw.reshape(4, 9 * ch, ch),
        cb,
        cp,
        co.reshape(1, ch),
        fw.reshape(4, 9 * ch, ch),
        fb,
        fp,
        regroup_matrix(batch, cc),
        regroup_matrix(batch, cf),
    )
    spread = spread_matrix(batch, cf)
    decoded = pl.pallas_call(
        functools.partial(raise_body, batch),
        grid=(rf,),
        out_shape=jax.ShapeDtypeStruct((batch, groups, 2 * rf, 2 * cf, ch), BF),
        in_specs=[
            pl.BlockSpec((rf + 2, cf + 2, SUB, ch), lambda r: (0, 0, 0, 0)),
            pl.BlockSpec(spread.shape, lambda r: (0, 0)),
            pl.BlockSpec((1, ch), lambda r: (0, 0)),
        ],
        out_specs=pl.BlockSpec((batch, groups, 2, 2 * cf, ch), lambda r: (0, 0, r, 0, 0)),
    )(z, spread, fo.reshape(1, ch))
    return decoded.reshape(batch, 2 * hf, 2 * cf, ch)


def solution(mesh):
    image = P(None, "row", "col", None)
    return jax.shard_map(
        per_device,
        mesh=mesh,
        in_specs=(image, image, image) + (P(),) * 8,
        out_specs=image,
        check_vma=False,
    )
```

profile of v0, /device:TPU:17, one launch (start us, length us, event | category | flops | bytes accessed | tf_op | source)
XLA Modules:
  0.0 55.6 jit_solution(10299687264090326947)
XLA Ops:
  0.0 48.5 %shard_map.136.z = bf16[10,18,16,256]{3,2,1,0:T(8,128)(2,1)} custom-call(bf16[4,4,4,8,256]{4,3,2,1,0:T(8,128)(2,1)} %bitcast.11, bf16[4,4,4,8,256]{4,3,2,1,0:T(8,128)(2,1)} %bitcast.12, bf16[4,4,8,16,256]{4,3,2,1,0:T(8,128)(2,1)} %bitcast.10, bf16[4,2304,256]{2,1,0:T(8,128)(2,1)} %bitcast.8, f32[4,256]{1,0:T(4,128)} %cb.1, bf16[256,256]{1,0:T(8,128)(2,1)} %cp.1, ...), custom_call_target="tpu_custom_call" | custom-call | tf_op jit(solution)/shard_map/pallas_call | solution.py:428
  48.5 7.1 %shard_map.137 = bf16[4,4,16,32,256]{4,3,2,1,0:T(8,128)(2,1)} custom-call(bf16[10,18,16,256]{3,2,1,0:T(8,128)(2,1)} %shard_map.136.z, bf16[512,288]{1,0:T(8,128)(2,1)} %constant.8.clone.spread, f32[1,256]{1,0:T(1,128)} %bitcast.14), custom_call_target="tpu_custom_call" | custom-call | tf_op jit(solution)/shard_map/pallas_call | solution.py:471
where the time goes:
time: 56.4 us; the launch traced here: 55.6 us
  Pallas kernels  55.6 us (99%)
    pallas_call x1, Pallas kernels, per_device(): pl.pallas_call(functools.partial(body, batch), out_shape=jax.ShapeDtypeSt...  48.5 us
    pallas_call x1, Pallas kernels, per_device(): pl.pallas_call(functools.partial(raise_body, batch), grid=(rf,), out_shap...  7.13 us

commit v1 on v0

--- a/solution.py
+++ b/solution.py
@@ -25,15 +25,16 @@
 
 
 class Level:
-    def __init__(self, images, stage, packed, landed, corners, send, recv):
+    def __init__(self, width, images, stage, packed, landed, corners, send, recv, slot):
+        self.width = width
         self.image = images.at[stage]
-        self.packed = packed.at[stage]
-        self.landed = landed.at[stage]
-        self.corners = corners.at[stage]
-        self.send = send.at[stage]
-        self.recv = recv.at[stage]
-        self.rows = images.shape[1] - 2
-        self.cols = images.shape[2] - 2
+        self.packed = packed.at[slot, :, 0:width]
+        self.landed = landed.at[slot, :, 0:width]
+        self.corners = corners.at[slot, :, 0:width, 0:width]
+        self.send = send.at[slot]
+        self.recv = recv.at[slot]
+        self.rows = images.shape[1] - 2 * width
+        self.cols = images.shape[2] - 2 * width
 
 
 class Place:
@@ -64,6 +65,14 @@
 
         return around(self.row, self.rows) * around(self.col, self.cols) - 1
 
+    def edges(self):
+        return (
+            self.row == 0,
+            self.row == self.rows - 1,
+            self.col == 0,
+            self.col == self.cols - 1,
+        )
+
     def at(self, dr, dc):
         return (self.row + dr, self.col + dc)
 
@@ -73,17 +82,19 @@
 
 
 def copies(place, lv):
-    r, c = lv.rows, lv.cols
+    r, c, h = lv.rows, lv.cols, lv.width
     im = lv.image
+    inner = pl.ds(h, r)
+    low, high_r, high_c = pl.ds(h, h), pl.ds(r, h), pl.ds(c, h)
     ends = (
-        (im.at[1 : r + 1, 1], im.at[1 : r + 1, c + 1]),
-        (im.at[1 : r + 1, c], im.at[1 : r + 1, 0]),
+        (im.at[inner, low], im.at[inner, pl.ds(c + h, h)]),
+        (im.at[inner, high_c], im.at[inner, pl.ds(0, h)]),
         (lv.packed.at[0], lv.landed.at[1]),
         (lv.packed.at[1], lv.landed.at[0]),
-        (im.at[1, 1], lv.corners.at[3]),
-        (im.at[1, c], lv.corners.at[2]),
-        (im.at[r, 1], lv.corners.at[1]),
-        (im.at[r, c], lv.corners.at[0]),
+        (im.at[low, low], lv.corners.at[3]),
+        (im.at[low, high_c], lv.corners.at[2]),
+        (im.at[high_r, low], lv.corners.at[1]),
+        (im.at[high_r, high_c], lv.corners.at[0]),
     )
     return [
         pltpu.make_async_remote_copy(
@@ -99,26 +110,27 @@
 
 
 def exchange(place, lv, batch):
-    r, c = lv.rows, lv.cols
+    r, c, h = lv.rows, lv.cols, lv.width
     groups = SUB // batch
     channels = lv.image.shape[-1]
     moves = copies(place, lv)
-    for i in (0, 1):
+    for i in (4, 5, 6, 7, 0, 1):
         pl.when(place.has(*DIRECTIONS[i]))(moves[i].start)
     slot = sub_index((c // groups, SUB, channels)) // batch
-    for side, row in ((0, 1), (1, r)):
-        v = lv.image[row, 1 : c + 1].astype(F32).reshape(c // groups, groups, SUB, channels)
-        total = None
-        for q in range(groups):
-            part = roll(v[:, q], batch * (q if side == 0 else q + 1))
-            total = part if total is None else jnp.where(slot == q, part, total)
-        lv.packed[side] = total.astype(BF)
-    for i in range(2, 8):
-        pl.when(place.has(*DIRECTIONS[i]))(moves[i].start)
+    for side in (0, 1):
+        for k in range(h):
+            row = h + k if side == 0 else r + k
+            v = lv.image[row, h : c + h].astype(F32).reshape(c // groups, groups, SUB, channels)
+            total = None
+            for q in range(groups):
+                part = roll(v[:, q], batch * (q if side == 0 else q + 1))
+                total = part if total is None else jnp.where(slot == q, part, total)
+            lv.packed[side, k] = total.astype(BF)
+        pl.when(place.has(*DIRECTIONS[2 + side]))(moves[2 + side].start)
 
 
 def settle(place, lv, batch, replicate):
-    r, c = lv.rows, lv.cols
+    r, c, h = lv.rows, lv.cols, lv.width
     im, landed, corners = lv.image, lv.landed, lv.corners
     groups = SUB // batch
     channels = im.shape[-1]
@@ -127,22 +139,19 @@
         pl.when(place.has(dr, dc))(moves[i].wait_send)
         pl.when(place.has(-dr, -dc))(moves[i].wait_recv)
 
-    no_up = place.row == 0
-    no_down = place.row == place.rows - 1
-    no_left = place.col == 0
-    no_right = place.col == place.cols - 1
+    no_up, no_down, no_left, no_right = place.edges()
 
     def rolled(tile, shift):
         return roll(tile.astype(F32), shift).astype(BF)
 
-    for missing, at, edge in ((no_left, 0, 1), (no_right, c + 1, c)):
+    for missing, at, edge in ((no_left, 0, h), (no_right, c + h, c)):
 
         @pl.when(missing)
         def _(at=at, edge=edge):
             if replicate:
-                im[1 : r + 1, at] = im[1 : r + 1, edge]
+                im[h : r + h, at : at + h] = im[h : r + h, edge : edge + h]
             else:
-                im[1 : r + 1, at] = jnp.zeros((r, SUB, channels), BF)
+                im[h : r + h, at : at + h] = jnp.zeros((r, h, SUB, channels), BF)
 
     for side, missing in ((0, no_up), (1, no_down)):
 
@@ -151,7 +160,7 @@
             if replicate:
                 landed[side] = lv.packed[side]
             else:
-                landed[side] = jnp.zeros((c // groups, SUB, channels), BF)
+                landed[side] = jnp.zeros((h, c // groups, SUB, channels), BF)
 
     last = c // groups - 1
     for k, vertical, horizontal in (
@@ -164,7 +173,7 @@
 
             @pl.when(jnp.logical_or(vertical, horizontal))
             def _(k=k):
-                corners[k] = jnp.zeros((SUB, channels), BF)
+                corners[k] = jnp.zeros((h, h, SUB, channels), BF)
 
         else:
             side = k // 2
@@ -174,42 +183,60 @@
 
             @pl.when(vertical)
             def _(k=k, turn=turn, row=row, col=col):
-                corners[k] = rolled(im[row, col], turn)
+                corners[k, 0, 0] = rolled(im[row, col], turn)
 
             shift = (-batch, 0, 0, batch)[k]
             block = 0 if k % 2 == 0 else last
 
             @pl.when(jnp.logical_and(jnp.logical_not(vertical), horizontal))
             def _(k=k, side=side, shift=shift, block=block):
-                corners[k] = rolled(landed[side, block], shift)
-
-    group = sub_index((c + 2, SUB, channels)) // batch
+                corners[k, 0, 0] = rolled(landed[side, 0, block], shift)
+
+    group = sub_index((c + 2 * h, SUB, channels)) // batch
     for side in (0, 1):
-        near = roll(im[r if side == 0 else 1].astype(F32), batch if side == 0 else -batch)
-        wide = landed[side].astype(F32)
-        parts = [
-            roll(wide, -batch * q if side == 0 else batch * (groups - 1 - q))
-            for q in range(groups)
-        ]
-        inner = jnp.stack(parts, axis=1).reshape(c, SUB, channels)
         turn = batch if side == 0 else -batch
-        ends = [
-            roll(corners[2 * side + k].astype(F32), turn).reshape(1, SUB, channels) for k in (0, 1)
-        ]
-        outer = jnp.concatenate([ends[0], inner, ends[1]], axis=0)
         chosen = 0 if side == 0 else groups - 1
-        im[0 if side == 0 else r + 1] = jnp.where(group == chosen, outer, near).astype(BF)
-
-
-def conv_rows(lv, weight, start, count):
-    c = lv.cols
-    channels = lv.image.shape[-1]
+        for k in range(h):
+            near = roll(im[r + k if side == 0 else h + k].astype(F32), turn)
+            wide = landed[side, k].astype(F32)
+            parts = [
+                roll(wide, -batch * q if side == 0 else batch * (groups - 1 - q))
+                for q in range(groups)
+            ]
+            inner = jnp.stack(parts, axis=1).reshape(c, SUB, channels)
+            ends = [roll(corners[2 * side + e, k].astype(F32), turn) for e in (0, 1)]
+            outer = jnp.concatenate([ends[0], inner, ends[1]], axis=0)
+            to = k if side == 0 else r + h + k
+            im[to] = jnp.where(group == chosen, outer, near).astype(BF)
+
+
+def clear_outside(place, ref, batch):
+    rows, cols, _, channels = ref.shape
+    no_up, no_down, no_left, no_right = place.edges()
+    for missing, at in ((no_left, 0), (no_right, cols - 1)):
+
+        @pl.when(missing)
+        def _(at=at):
+            ref[:, at] = jnp.zeros((rows, SUB, channels), BF)
+
+    group = sub_index((cols, SUB, channels)) // batch
+    for missing, at, chosen in ((no_up, 0, 0), (no_down, rows - 1, SUB // batch - 1)):
+
+        @pl.when(missing)
+        def _(at=at, chosen=chosen):
+            ref[at] = jnp.where(group == chosen, 0.0, ref[at].astype(F32)).astype(BF)
+
+
+def conv_rows(image, weight, start, count):
+    c = image.shape[1] - 2
+    channels = image.shape[-1]
     taps = [
-        lv.image[pl.ds(start + dr, count), dc : dc + c].reshape(count * c * SUB, channels)
+        image[pl.ds(start + dr, count), dc : dc + c].reshape(count * c * SUB, channels)
         for dr in range(3)
         for dc in range(3)
     ]
-    return jnp.dot(jnp.concatenate(taps, axis=1), weight[...], preferred_element_type=F32)
+    v = jnp.dot(jnp.concatenate(taps, axis=1), weight[...], preferred_element_type=F32)
+    return v
 
 
 def body(
@@ -229,6 +256,10 @@
     out,
     ic,
     if_,
+    hid_c,
+    hid_f,
+    up_c,
+    up_f,
     pack_c,
     pack_f,
     land_c,
@@ -252,7 +283,7 @@
     for i in range(4):
         for k, (src, dst) in enumerate(((cw_hbm, cw), (fw_hbm, fw))):
             loads[k, i] = pltpu.make_async_copy(src.at[i], dst.at[i], wsem.at[k, i])
-    for key in ((0, 0), (1, 0), (0, 1), (1, 1), (0, 2), (0, 3), (1, 2), (1, 3)):
+    for key in ((0, 0), (0, 1), (1, 0), (0, 2), (0, 3), (1, 1), (1, 2), (1, 3)):
         loads[key].start()
 
     barrier = pltpu.get_barrier_semaphore()
@@ -264,8 +295,10 @@
                 barrier, inc=1, device_id=place.at(*d), device_id_type=pl.DeviceIdType.MESH
             )
 
-    lc = [Level(ic, s, pack_c, land_c, corner_c, send_c, recv_c) for s in range(5)]
-    lf = [Level(if_, s, pack_f, land_f, corner_f, send_f, recv_f) for s in range(5)]
+    side_c = (pack_c, land_c, corner_c, send_c, recv_c)
+    side_f = (pack_f, land_f, corner_f, send_f, recv_f)
+    lc = [Level(2, ic, 0, *side_c, 0), Level(2, ic, 1, *side_c, 1), Level(1, up_c, 0, *side_c, 2)]
+    lf = [Level(2, if_, 0, *side_f, 0), Level(2, if_, 1, *side_f, 1), Level(1, up_f, 0, *side_f, 2)]
     rc, cc, rf, cf = lc[0].rows, lc[0].cols, lf[0].rows, lf[0].cols
 
     def regroup(ref, perm, row):
@@ -276,8 +309,7 @@
     def _(row):
         v = regroup(skip_c, perm_c, row)
         xc[row] = v + regroup(prev, perm_c, row)
-        ic[0, row + 1, 1 : cc + 1] = jnp.maximum(v, 0.0).astype(BF)
-
+        ic[0, row + 2, 2 : cc + 2] = jnp.maximum(v, 0.0).astype(BF)
 
     pl.semaphore_wait(barrier, place.peers())
 
@@ -287,32 +319,47 @@
     def _(row):
         v = regroup(skip_f, perm_f, row)
         xf[row] = v.astype(BF)
-        if_[0, row + 1, 1 : cf + 1] = jnp.maximum(v, 0.0).astype(BF)
+        if_[0, row + 2, 2 : cf + 2] = jnp.maximum(v, 0.0).astype(BF)
 
     exchange(place, lf[0], batch)
 
     def coarse(stage, finish):
         settle(place, lc[stage], batch, False)
-        loads[0, stage].wait()
-        v = conv_rows(lc[stage], cw.at[stage], 0, rc) + cb[stage : stage + 1]
-        v = finish(v.reshape(rc, cc, SUB, channels))
-        lc[stage + 1].image[1 : rc + 1, 1 : cc + 1] = v
+        first = 2 * stage
+        loads[0, first].wait()
+        v = conv_rows(lc[stage].image, cw.at[first], 0, rc + 2) + cb[first : first + 1]
+        hid_c[...] = jnp.maximum(v, 0.0).astype(BF).reshape(rc + 2, cc + 2, SUB, channels)
+        clear_outside(place, hid_c, batch)
+        loads[0, first + 1].wait()
+        v = conv_rows(hid_c, cw.at[first + 1], 0, rc) + cb[first + 1 : first + 2]
+        lc[stage + 1].image[finish[0] : finish[0] + rc, finish[0] : finish[0] + cc] = finish[1](
+            v.reshape(rc, cc, SUB, channels)
+        )
         exchange(place, lc[stage + 1], batch)
 
     step = 2 if rf % 2 == 0 else 1
 
-    def fine(stage, finish, first, last):
-        @pl.loop(first, last)
+    def fine_hidden(stage):
+        settle(place, lf[stage], batch, False)
+        first = 2 * stage
+        loads[1, first].wait()
+
+        @pl.loop(0, (rf + 2) // step)
         def _(i):
-            v = conv_rows(lf[stage], fw.at[stage], i * step, step) + fb[stage : stage + 1]
+            v = conv_rows(lf[stage].image, fw.at[first], i * step, step) + fb[first : first + 1]
+            v = jnp.maximum(v, 0.0).astype(BF)
+            hid_f[pl.ds(i * step, step)] = v.reshape(step, cf + 2, SUB, channels)
+
+        clear_outside(place, hid_f, batch)
+
+    def fine_final(stage, finish):
+        second = 2 * stage + 1
+        loads[1, second].wait()
+
+        @pl.loop(0, rf // step)
+        def _(i):
+            v = conv_rows(hid_f, fw.at[second], i * step, step) + fb[second : second + 1]
             finish(i * step, v.reshape(step, cf, SUB, channels))
-
-    def fine_ready(stage):
-        settle(place, lf[stage], batch, False)
-        loads[1, stage].wait()
-
-    def hidden(v):
-        return jnp.maximum(v, 0.0).astype(BF)
 
     def summed(v):
         v = v + xc[...]
@@ -324,39 +371,25 @@
         z = jnp.dot(top, cp[...], preferred_element_type=F32)
         return z.astype(BF).reshape(rc, cc, SUB, channels)
 
-    def keep_hidden(stage):
-        def finish(row, v):
-            if_[stage + 1, pl.ds(row + 1, step), 1 : cf + 1] = hidden(v)
-
-        return finish
-
     def keep_unit(row, v):
         sum_f[pl.ds(row, step)] = v + xf[pl.ds(row, step)].astype(F32)
 
     def keep_top(row, v):
         top = (v + sum_f[pl.ds(row, step)]).astype(BF).reshape(step * cf * SUB, channels)
         z = jnp.dot(top, fp[...], preferred_element_type=F32)
-        if_[4, pl.ds(row + 1, step), 1 : cf + 1] = z.astype(BF).reshape(step, cf, SUB, channels)
-
-    steps = rf // step
-    half = steps // 2
-    coarse(0, hidden)
-    fine_ready(0)
-    fine(0, keep_hidden(0), 0, steps)
-    exchange(place, lf[1], batch)
-    coarse(1, summed)
-    fine_ready(1)
-    fine(1, keep_unit, 0, half)
-    coarse(2, hidden)
-    fine(1, keep_unit, half, steps)
-    coarse(3, lifted)
-    settle(place, lc[4], batch, True)
+        up_f[0, pl.ds(row + 1, step), 1 : cf + 1] = z.astype(BF).reshape(step, cf, SUB, channels)
+
+    coarse(0, (2, summed))
+    fine_hidden(0)
+    coarse(1, (1, lifted))
+    fine_final(0, keep_unit)
+    settle(place, lc[2], batch, True)
 
     @pl.loop(0, rc)
     def _(row):
-        mid = 0.75 * ic[4, row + 1].astype(F32)
+        mid = 0.75 * up_c[0, row + 1].astype(F32)
         for p in range(2):
-            v = mid + 0.25 * ic[4, row + 2 * p].astype(F32)
+            v = mid + 0.25 * up_c[0, row + 2 * p].astype(F32)
             core = 0.75 * v[1 : cc + 1]
             even = core + 0.25 * v[0:cc]
             odd = core + 0.25 * v[2 : cc + 2]
@@ -364,20 +397,17 @@
             joined = (both + co[...]).astype(BF).astype(F32)
             total = joined + sum_f[2 * row + p]
             sum_f[2 * row + p] = total
-            if_[2, 2 * row + p + 1, 1 : cf + 1] = jnp.maximum(total, 0.0).astype(BF)
-
+            if_[1, 2 * row + p + 2, 2 : cf + 2] = jnp.maximum(total, 0.0).astype(BF)
+
+    exchange(place, lf[1], batch)
+    fine_hidden(1)
+    fine_final(1, keep_top)
     exchange(place, lf[2], batch)
-    fine_ready(2)
-    fine(2, keep_hidden(2), 0, steps)
-    exchange(place, lf[3], batch)
-    fine_ready(3)
-    fine(3, keep_top, 0, steps)
-    exchange(place, lf[4], batch)
-    settle(place, lf[4], batch, True)
+    settle(place, lf[2], batch, True)
 
     @pl.loop(0, rf + 2)
     def _(row):
-        out[row] = if_[4, row]
+        out[row] = up_f[0, row]
 
 
 def raise_body(batch, z, spread, offset, out):
@@ -431,23 +461,27 @@
         in_specs=[vmem, vmem, vmem, hbm, vmem, vmem, vmem, hbm, vmem, vmem, vmem, vmem],
         out_specs=vmem,
         scratch_shapes=[
-            pltpu.VMEM((5, rc + 2, cc + 2, SUB, ch), BF),
-            pltpu.VMEM((5, rf + 2, cf + 2, SUB, ch), BF),
-            pltpu.VMEM((5, 2, cc // groups, SUB, ch), BF),
-            pltpu.VMEM((5, 2, cf // groups, SUB, ch), BF),
-            pltpu.VMEM((5, 2, cc // groups, SUB, ch), BF),
-            pltpu.VMEM((5, 2, cf // groups, SUB, ch), BF),
-            pltpu.VMEM((5, 4, SUB, ch), BF),
-            pltpu.VMEM((5, 4, SUB, ch), BF),
+            pltpu.VMEM((2, rc + 4, cc + 4, SUB, ch), BF),
+            pltpu.VMEM((2, rf + 4, cf + 4, SUB, ch), BF),
+            pltpu.VMEM((rc + 2, cc + 2, SUB, ch), BF),
+            pltpu.VMEM((rf + 2, cf + 2, SUB, ch), BF),
+            pltpu.VMEM((1, rc + 2, cc + 2, SUB, ch), BF),
+            pltpu.VMEM((1, rf + 2, cf + 2, SUB, ch), BF),
+            pltpu.VMEM((3, 2, 2, cc // groups, SUB, ch), BF),
+            pltpu.VMEM((3, 2, 2, cf // groups, SUB, ch), BF),
+            pltpu.VMEM((3, 2, 2, cc // groups, SUB, ch), BF),
+            pltpu.VMEM((3, 2, 2, cf // groups, SUB, ch), BF),
+            pltpu.VMEM((3, 4, 2, 2, SUB, ch), BF),
+            pltpu.VMEM((3, 4, 2, 2, SUB, ch), BF),
             pltpu.VMEM((4, 9 * ch, ch), BF),
             pltpu.VMEM((4, 9 * ch, ch), BF),
             pltpu.VMEM((rc, cc, SUB, ch), F32),
             pltpu.VMEM((rf, cf, SUB, ch), BF),
             pltpu.VMEM((rf, cf, SUB, ch), F32),
-            dma((5, 8)),
-            dma((5, 8)),
-            dma((5, 8)),
-            dma((5, 8)),
+            dma((3, 8)),
+            dma((3, 8)),
+            dma((3, 8)),
+            dma((3, 8)),
             dma((2, 4)),
         ],
         compiler_params=pltpu.CompilerParams(

time: 56.4 us -> 52.8 us (0.936); the launches traced: 55.6 us -> 52.6 us
  Pallas kernels: 55.6 us -> 52.6 us
    pallas_call x1, Pallas kernels: 48.5 us -> 45.4 us  [per_device(): pl.pallas_call(functools.partial(body, batch), out_shape=jax.ShapeDtypeSt...]
where the time goes in v1:
time: 52.8 us; the launch traced here: 52.6 us
  Pallas kernels  52.6 us (100%)
    pallas_call x1, Pallas kernels, per_device(): pl.pallas_call(functools.partial(body, batch), out_shape=jax.ShapeDtypeSt...  45.4 us
    pallas_call x1, Pallas kernels, per_device(): pl.pallas_call(functools.partial(raise_body, batch), grid=(rf,), out_shap...  7.14 us

profile of v1, /device:TPU:17, one launch (start us, length us, event | category | flops | bytes accessed | tf_op | source)
XLA Modules:
  0.0 52.6 jit_solution(459559057842957953)
XLA Ops:
  0.0 45.4 %shard_map.136.z = bf16[10,18,16,256]{3,2,1,0:T(8,128)(2,1)} custom-call(bf16[4,4,4,8,256]{4,3,2,1,0:T(8,128)(2,1)} %bitcast.11, bf16[4,4,4,8,256]{4,3,2,1,0:T(8,128)(2,1)} %bitcast.12, bf16[4,4,8,16,256]{4,3,2,1,0:T(8,128)(2,1)} %bitcast.10, bf16[4,2304,256]{2,1,0:T(8,128)(2,1)} %bitcast.8, f32[4,256]{1,0:T(4,128)} %cb.1, bf16[256,256]{1,0:T(8,128)(2,1)} %cp.1, ...), custom_call_target="tpu_custom_call" | custom-call | tf_op jit(solution)/shard_map/pallas_call | solution.py:458
  45.5 7.1 %shard_map.137 = bf16[4,4,16,32,256]{4,3,2,1,0:T(8,128)(2,1)} custom-call(bf16[10,18,16,256]{3,2,1,0:T(8,128)(2,1)} %shard_map.136.z, bf16[512,288]{1,0:T(8,128)(2,1)} %constant.8.clone.spread, f32[1,256]{1,0:T(1,128)} %bitcast.14), custom_call_target="tpu_custom_call" | custom-call | tf_op jit(solution)/shard_map/pallas_call | solution.py:505

commit v2 on v1

--- a/solution.py
+++ b/solution.py
@@ -227,16 +227,21 @@
             ref[at] = jnp.where(group == chosen, 0.0, ref[at].astype(F32)).astype(BF)
 
 
-def conv_rows(image, weight, start, count):
-    c = image.shape[1] - 2
+def conv_rows(image, weight, start, count, spans=None):
     channels = image.shape[-1]
+    spans = spans or ((0, image.shape[1] - 2),)
     taps = [
-        image[pl.ds(start + dr, count), dc : dc + c].reshape(count * c * SUB, channels)
+        jnp.concatenate(
+            [
+                image[pl.ds(start + dr, count), at + dc : at + dc + n].reshape(-1, channels)
+                for at, n in spans
+            ],
+            axis=0,
+        )
         for dr in range(3)
         for dc in range(3)
     ]
-    v = jnp.dot(jnp.concatenate(taps, axis=1), weight[...], preferred_element_type=F32)
-    return v
+    return jnp.dot(jnp.concatenate(taps, axis=1), weight[...], preferred_element_type=F32)
 
 
 def body(
@@ -340,16 +345,31 @@
     step = 2 if rf % 2 == 0 else 1
 
     def fine_hidden(stage):
+        first = 2 * stage
+
+        def compute(start, count, spans):
+            v = conv_rows(lf[stage].image, fw.at[first], start, count, spans)
+            v = jnp.maximum(v + fb[first : first + 1], 0.0).astype(BF)
+            done = 0
+            for at, n in spans:
+                size = count * n * SUB
+                part = v[done : done + size].reshape(count, n, SUB, channels)
+                hid_f[pl.ds(start, count), at : at + n] = part
+                done += size
+
+        loads[1, first].wait()
+
+        @pl.loop(0, (rf - 2) // step)
+        def _(i):
+            compute(2 + i * step, step, ((2, cf - 2),))
+
         settle(place, lf[stage], batch, False)
-        first = 2 * stage
-        loads[1, first].wait()
-
-        @pl.loop(0, (rf + 2) // step)
+
+        @pl.loop(0, 2)
         def _(i):
-            v = conv_rows(lf[stage].image, fw.at[first], i * step, step) + fb[first : first + 1]
-            v = jnp.maximum(v, 0.0).astype(BF)
-            hid_f[pl.ds(i * step, step)] = v.reshape(step, cf + 2, SUB, channels)
-
+            compute(i * rf, 2, ((0, cf + 2),))
+
+        compute(2, rf - 2, ((0, 2), (cf, 2)))
         clear_outside(place, hid_f, batch)
 
     def fine_final(stage, finish):

time: 52.8 us -> 51.8 us (0.981)
  Pallas kernels: 52.6 us -> 51.7 us
    pallas_call x1, Pallas kernels: 45.4 us -> 44.5 us  [per_device(): pl.pallas_call(functools.partial(body, batch), out_shape=jax.ShapeDtypeSt...]
where the time goes in v2:
time: 51.8 us; the launch traced here: 51.7 us
  Pallas kernels  51.7 us (100%)
    pallas_call x1, Pallas kernels, per_device(): pl.pallas_call(functools.partial(body, batch), out_shape=jax.ShapeDtypeSt...  44.5 us
    pallas_call x1, Pallas kernels, per_device(): pl.pallas_call(functools.partial(raise_body, batch), grid=(rf,), out_shap...  7.13 us

profile of v2, /device:TPU:17, one launch (start us, length us, event | category | flops | bytes accessed | tf_op | source)
XLA Modules:
  0.0 51.7 jit_solution(12084826998672788975)
XLA Ops:
  0.0 44.5 %shard_map.136.z = bf16[10,18,16,256]{3,2,1,0:T(8,128)(2,1)} custom-call(bf16[4,4,4,8,256]{4,3,2,1,0:T(8,128)(2,1)} %bitcast.11, bf16[4,4,4,8,256]{4,3,2,1,0:T(8,128)(2,1)} %bitcast.12, bf16[4,4,8,16,256]{4,3,2,1,0:T(8,128)(2,1)} %bitcast.10, bf16[4,2304,256]{2,1,0:T(8,128)(2,1)} %bitcast.8, f32[4,256]{1,0:T(4,128)} %cb.1, bf16[256,256]{1,0:T(8,128)(2,1)} %cp.1, ...), custom_call_target="tpu_custom_call" | custom-call | tf_op jit(solution)/shard_map/pallas_call | solution.py:478
  44.5 7.1 %shard_map.137 = bf16[4,4,16,32,256]{4,3,2,1,0:T(8,128)(2,1)} custom-call(bf16[10,18,16,256]{3,2,1,0:T(8,128)(2,1)} %shard_map.136.z, bf16[512,288]{1,0:T(8,128)(2,1)} %constant.8.clone.spread, f32[1,256]{1,0:T(1,128)} %bitcast.14), custom_call_target="tpu_custom_call" | custom-call | tf_op jit(solution)/shard_map/pallas_call | solution.py:525
